TPU v7x, 32 devices: a whole 2x2x4 slice. The times are simulated.
32 devices in a mesh: dp: 16 (over z, y, core), tensor: 2 (over x).
Axes of the slice: x: 2, y: 2, z: 4, core: 2. Of those that a mesh axis runs over, the one named last changes fastest.
Arguments:
- expert_act: bfloat16 [16384, 2880], P(('dp', 'tensor')), may hold values from -6 to 6
- grad_out: bfloat16 [32768, 1440], P(('dp', 'tensor')), may hold values from -6 to 6
- slot_token: int32 [16384], P(('dp', 'tensor')), may hold values from 0 to 1023, as said below
- slot_prob: float32 [16384], P(('dp', 'tensor')), may hold values from 0.2 to 1
- live_count: int32 [32], P(('dp', 'tensor')), may hold values from 128 to 512, as said below
Outputs:
- weight_grad: float32 [2880, 1440], P('dp', 'tensor')
Inputs may be any that keep to these rules, and one draw needn't show every extreme that they name: `slot_token`: each device's 512 entries are distinct token indices of that device. `live_count`: each entry is 512 // j for some j of 1 to 4.
All inputs are finite; a program needn't handle non-finite values.
Results may differ from a plain program's by a relative error of at most 0.0029.
Values may be sent and summed in bfloat16 or wider, within the bound.
A program may use at most 128 MiB of HBM per device.

v0:
```python
import functools
import math

import jax
import jax.numpy as jnp
from jax import lax
from jax.experimental import pallas as pl
from jax.experimental.pallas import tpu as pltpu
from jax.sharding import PartitionSpec as P

MESH = pl.DeviceIdType.MESH


def kernel(
    outer,
    acts_hbm, grad_hbm, token_ref, prob_ref, live_ref, out_ref,
    acts_raw, grad_raw, acts, peer_acts, mine, peer,
    send_a, recv_a, send_b, recv_b, send_z, recv_z,
    load_sems, pair_sems, a_sems, b_sems, z_sems,
):
    dp = lax.axis_index("dp")
    half = lax.axis_index("tensor")
    core = lax.rem(dp, 2)
    mid = lax.rem(dp // 2, 2)
    own = dp // 4
    my_a = half * (1 - core) + mid * core
    my_b = mid * (1 - core) + half * core
    flip_mid = dp + 2 - 4 * mid
    pair_dev = {"dp": dp + 1 - 2 * core, "tensor": half}
    a_dev = {
        "dp": dp * (1 - core) + flip_mid * core,
        "tensor": (1 - half) * (1 - core) + half * core,
    }
    b_dev = {
        "dp": flip_mid * (1 - core) + dp * core,
        "tensor": half * (1 - core) + (1 - half) * core,
    }

    def z_dev(step):
        return {"dp": dp + (target(step) - own) * 4, "tensor": half}

    def target(step):
        offset = outer // 2 + step // 2 - (step % 2) * step
        return lax.rem(own + offset, outer)

    def remote(src, dst, sems, device):
        return pltpu.make_async_remote_copy(
            src_ref=src, dst_ref=dst, send_sem=sems[0], recv_sem=sems[1],
            device_id=device, device_id_type=MESH,
        )

    grad_order = (1 - half, half)
    load_grads = [
        pltpu.make_async_copy(grad_hbm.at[g], grad_raw.at[g], load_sems.at[outer + i])
        for i, g in enumerate(grad_order)
    ]

    def load_acts(step):
        o = target(step)
        return pltpu.make_async_copy(acts_hbm.at[o], acts_raw.at[o], load_sems.at[step])

    load_grads[0].start()
    load_acts(0).start()

    barrier = pltpu.get_barrier_semaphore()
    for device in [pair_dev, a_dev, b_dev] + [z_dev(s) for s in range(outer - 1)]:
        pl.semaphore_signal(barrier, inc=1, device_id=device, device_id_type=MESH)

    slots, tokens = token_ref.shape[1], grad_raw.shape[2]
    chosen = lax.broadcasted_iota(jnp.int32, (tokens, slots), 0) == token_ref[...]
    onehot = jnp.where(chosen, 1.0, 0.0).astype(jnp.bfloat16)
    live = lax.broadcasted_iota(jnp.int32, (1, slots), 1) < live_ref[0]
    weight = jnp.where(live, prob_ref[...], 0.0)
    rows = acts.shape[3]

    def copy_grad(i):
        g = grad_order[i]
        return remote(
            mine.at[g], peer.at[g],
            (pair_sems.at[0, outer + i], pair_sems.at[1, outer + i]), pair_dev,
        )

    def copy_acts(step):
        o = target(step)
        return remote(
            acts.at[1 - core, o], peer_acts.at[o],
            (pair_sems.at[0, step], pair_sems.at[1, step]), pair_dev,
        )

    def weigh(i):
        g = grad_order[i]
        picked = jnp.dot(grad_raw[g], onehot, preferred_element_type=jnp.float32)
        mine[g] = (picked * weight).astype(jnp.bfloat16)

    def divide(step):
        o = target(step)
        load_acts(step).wait()
        for k in range(4):
            acts[k % 2, o, k // 2] = acts_raw[o, k * rows : (k + 1) * rows, :]

    load_grads[0].wait()
    load_grads[1].start()
    weigh(0)
    for step in range(1, outer):
        load_acts(step).start()
    pl.semaphore_wait(barrier, outer + 2)
    copy_grad(0).start()
    divide(0)
    copy_acts(0).start()
    load_grads[1].wait()
    weigh(1)
    copy_grad(1).start()

    def feed(step, carry):
        divide(step)
        copy_acts(step).start()
        return carry

    lax.fori_loop(1, outer, feed, 0)
    copy_grad(0).wait_recv()

    def contract(left, right):
        return lax.dot_general(
            left, right, (((1,), (1,)), ((), ())), preferred_element_type=jnp.float32
        )

    def term(step, a, b):
        o, m = target(step), b * (1 - core) + a * core
        column = a * (1 - core) + b * core
        return contract(acts[core, o, m], mine[column]) + contract(
            peer_acts[o, m], peer[column]
        )

    def copy_a(step, k):
        return remote(
            send_a.at[step, k], recv_a.at[step, k],
            (a_sems.at[0, step, k], a_sems.at[1, step, k]), a_dev,
        )

    def copy_b(step):
        return remote(
            send_b.at[step], recv_b.at[step],
            (b_sems.at[0, step], b_sems.at[1, step]), b_dev,
        )

    def copy_z(step):
        return remote(
            send_z.at[step], recv_z.at[step],
            (z_sems.at[0, step], z_sems.at[1, step]), z_dev(step),
        )

    def first(step, k):
        b = 1 - my_b if k == 0 else my_b
        send_a[step, k] = term(step, 1 - my_a, b).astype(jnp.bfloat16)
        copy_a(step, k).start()

    def second(step):
        total = term(step, my_a, 1 - my_b)
        copy_a(step, 0).wait_recv()
        total = total + recv_a[step, 0].astype(jnp.float32)
        send_b[step] = total.astype(jnp.bfloat16)
        copy_b(step).start()

    def third(step):
        total = term(step, my_a, my_b)
        copy_a(step, 1).wait_recv()
        total = total + recv_a[step, 1].astype(jnp.float32)
        copy_b(step).wait_recv()
        total = total + recv_b[step].astype(jnp.float32)
        send_z[step] = total.astype(jnp.bfloat16)
        copy_z(step).start()

    def stage(step, carry):
        @pl.when(step < outer)
        def _():
            copy_acts(step).wait_recv()
            first(step, 0)

        @pl.when(step == 1)
        def _():
            copy_grad(1).wait_recv()

        @pl.when((step >= 1) & (step <= outer))
        def _():
            first(step - 1, 1)

        @pl.when(step >= 2)
        def _():
            second(step - 2)

        @pl.when(step >= 3)
        def _():
            third(step - 3)

        return carry

    lax.fori_loop(0, outer + 2, stage, 0)
    last = outer - 1
    out_ref[...] = term(last, my_a, my_b)

    def add(step, carry):
        copy_z(step).wait_recv()
        out_ref[...] += recv_z[step].astype(jnp.float32)
        return carry

    lax.fori_loop(0, last, add, 0)
    copy_a(last, 1).wait_recv()
    out_ref[...] += recv_a[last, 1].astype(jnp.float32)
    copy_b(last).wait_recv()
    out_ref[...] += recv_b[last].astype(jnp.float32)

    def drain(step, carry):
        copy_acts(step).wait_send()
        copy_a(step, 0).wait_send()
        copy_a(step, 1).wait_send()
        copy_b(step).wait_send()
        return carry

    lax.fori_loop(0, outer, drain, 0)

    def drain_z(step, carry):
        copy_z(step).wait_send()
        return carry

    lax.fori_loop(0, outer - 1, drain_z, 0)
    copy_grad(0).wait_send()
    copy_grad(1).wait_send()


def shards(expert_act, grad_out, slot_token, slot_prob, live_count):
    slots, hidden = expert_act.shape
    tokens = grad_out.shape[0]
    ranks, halves = lax.axis_size("dp"), lax.axis_size("tensor")
    outer = ranks // 4
    rows, columns = hidden // ranks, grad_out.shape[1] // halves
    scaling = 1.0 / math.sqrt(slots * ranks * halves)
    bf16, dma = jnp.bfloat16, pltpu.SemaphoreType.DMA
    total = pl.pallas_call(
        functools.partial(kernel, outer),
        out_shape=jax.ShapeDtypeStruct((rows, columns), jnp.float32),
        in_specs=[
            pl.BlockSpec(memory_space=pl.ANY),
            pl.BlockSpec(memory_space=pl.ANY),
            pl.BlockSpec(memory_space=pltpu.VMEM),
            pl.BlockSpec(memory_space=pltpu.VMEM),
            pl.BlockSpec(memory_space=pltpu.SMEM),
        ],
        out_specs=pl.BlockSpec(memory_space=pltpu.VMEM),
        scratch_shapes=[
            pltpu.VMEM((outer, 4 * rows, slots), bf16),
            pltpu.VMEM((halves, columns, tokens), bf16),
            pltpu.VMEM((2, outer, 2, rows, slots), bf16),
            pltpu.VMEM((outer, 2, rows, slots), bf16),
            pltpu.VMEM((halves, columns, slots), bf16),
            pltpu.VMEM((halves, columns, slots), bf16),
            pltpu.VMEM((outer, 2, rows, columns), bf16),
            pltpu.VMEM((outer, 2, rows, columns), bf16),
            pltpu.VMEM((outer, rows, columns), bf16),
            pltpu.VMEM((outer, rows, columns), bf16),
            pltpu.VMEM((outer - 1, rows, columns), bf16),
            pltpu.VMEM((outer - 1, rows, columns), bf16),
            dma((outer + 2,)),
            dma((2, outer + 2)),
            dma((2, outer, 2)),
            dma((2, outer)),
            dma((2, outer - 1)),
        ],
        compiler_params=pltpu.CompilerParams(
            collective_id=0, has_side_effects=True, vmem_limit_bytes=53 * 2**20
        ),
    )(
        expert_act.T.reshape(outer, 4 * rows, slots),
        grad_out.T.reshape(halves, columns, tokens),
        slot_token[None, :],
        slot_prob[None, :],
        live_count,
    )
    return total * scaling


def solution(mesh):
    return jax.shard_map(
        shards,
        mesh=mesh,
        in_specs=(
            P(("dp", "tensor"), None),
            P(("dp", "tensor"), None),
            P(("dp", "tensor")),
            P(("dp", "tensor")),
            P(("dp", "tensor")),
        ),
        out_specs=P("dp", "tensor"),
        check_vma=False,
    )
```

profile of v0, /device:TPU:0, one launch (start us, length us, event | category | flops | bytes accessed | tf_op | source)
XLA Modules:
  0.0 53.0 jit_solution(2812924463170082394)
XLA Ops:
  0.7 0.0 copy-start
  0.7 0.7 %copy-done = s32[512]{0:T(512)S(1)} copy-done((s32[512]{0:T(512)S(1)}, s32[512]{0:T(512)}, u32[]{:S(2)}) %copy-start) | copy-done | bytes 2072
  1.3 0.0 copy-start.1
  1.3 0.7 %copy-done.1 = f32[512]{0:T(512)S(1)} copy-done((f32[512]{0:T(512)S(1)}, f32[512]{0:T(512)}, u32[]{:S(2)}) %copy-start.1) | copy-done | bytes 2072
  2.0 50.1 %shard_map.55 = f32[180,720]{1,0:T(8,128)S(1)} custom-call(bf16[4,720,512]{2,1,0:T(8,128)(2,1)} %bitcast.10, bf16[2,720,1024]{2,1,0:T(8,128)(2,1)} %bitcast.11, s32[1,512]{1,0:T(1,128)S(1)} %bitcast.8, f32[1,512]{1,0:T(1,128)S(1)} %bitcast.9, s32[1]{0:T(128)S(6)} %copy.6.live_ref), custom_call_target="tpu_custom_call" | custom-call | tf_op jit(solution)/shard_map/pallas_call | solution.py:238
  52.1 0.8 %broadcast_multiply_fusion = f32[180,720]{1,0:T(8,128)} fusion(f32[180,720]{1,0:T(8,128)S(1)} %shard_map.55), kind=kLoop, calls=%fused_computation | loop fusion | flops 129600 | bytes 1036800 | tf_op jit(solution)/shard_map/mul | solution.py:278
Async XLA Ops:
  0.7 0.7 %copy-start = (s32[512]{0:T(512)S(1)}, s32[512]{0:T(512)}, u32[]{:S(2)}) copy-start(s32[512]{0:T(512)} %param.7) | copy-start | bytes 6148
  1.3 0.7 %copy-start.1 = (f32[512]{0:T(512)S(1)}, f32[512]{0:T(512)}, u32[]{:S(2)}) copy-start(f32[512]{0:T(512)} %param.8) | copy-start | bytes 6148
where the time goes:
time: 53.2 us; the launch traced here: 53 us
  Pallas kernels  50.1 us (94%)
  local copies, waits for them, and re-layouts  1.36 us (3%)
  other arithmetic  0.85 us (2%)
  between operations  0.67 us (1%)
    pallas_call x1, Pallas kernels, shards(): pl.pallas_call(functools.partial(kernel, outer), out_shape=jax.ShapeDtype...  50.1 us
    unnamed x4, local copies, waits for them, and re-layouts  1.36 us

commit v1 on v0

v1 whole, which is shorter than its diff:
```python
import functools
import math

import jax
import jax.numpy as jnp
from jax import lax
from jax.experimental import pallas as pl
from jax.experimental.pallas import tpu as pltpu
from jax.sharding import PartitionSpec as P

MESH = pl.DeviceIdType.MESH
LANES = 128


def kernel(
    outer, wide,
    acts_hbm, grad_hbm, token_hbm, prob_hbm, live_ref, out_ref,
    token_ref, prob_ref, acts_raw, grad_raw, rest_raw, acts, peer_acts,
    mine, peer, mine_rest, peer_rest,
    send_a, recv_a, send_b, recv_b, send_z, recv_z,
    send_r, recv_r, own_r, send_p, recv_p, turned,
    small_sems, load_sems, grad_sems, acts_sems, w_sems,
    a_sems, b_sems, z_sems, r_sems, p_sems,
):
    dp = lax.axis_index("dp")
    half = lax.axis_index("tensor")
    core = lax.rem(dp, 2)
    mid = lax.rem(dp // 2, 2)
    own = dp // 4
    my_a = half * (1 - core) + mid * core
    my_b = mid * (1 - core) + half * core
    flip_mid = dp + 2 - 4 * mid
    pair_dev = {"dp": dp + 1 - 2 * core, "tensor": half}
    x_dev = {"dp": dp, "tensor": 1 - half}
    y_dev = {"dp": flip_mid, "tensor": half}
    xy_dev = {"dp": flip_mid, "tensor": 1 - half}
    a_dev = {
        "dp": dp * (1 - core) + flip_mid * core,
        "tensor": (1 - half) * (1 - core) + half * core,
    }
    b_dev = {
        "dp": flip_mid * (1 - core) + dp * core,
        "tensor": half * (1 - core) + (1 - half) * core,
    }
    last = outer - 1
    rows = acts.shape[3]
    rest = rest_raw.shape[0] // 2

    def target(step):
        offset = outer // 2 + step // 2 - (step % 2) * step
        return lax.rem(own + offset, outer)

    def z_dev(step):
        return {"dp": dp + (target(step) - own) * 4, "tensor": half}

    def remote(src, dst, send, recv, device):
        return pltpu.make_async_remote_copy(
            src_ref=src, dst_ref=dst, send_sem=send, recv_sem=recv,
            device_id=device, device_id_type=MESH,
        )

    grad_order = (1 - half, half)
    load_small = [
        pltpu.make_async_copy(token_hbm, token_ref, small_sems.at[0]),
        pltpu.make_async_copy(prob_hbm, prob_ref, small_sems.at[1]),
    ]
    load_wide = [
        pltpu.make_async_copy(
            grad_hbm.at[g, pl.ds(0, wide)], grad_raw.at[g], grad_sems.at[i]
        )
        for i, g in enumerate(grad_order)
    ]
    load_rest = [
        pltpu.make_async_copy(
            grad_hbm.at[g, pl.ds(wide, rest)], rest_raw.at[pl.ds(g * rest, rest)],
            grad_sems.at[2 + g],
        )
        for g in range(2)
    ]

    def load_acts(step):
        o = target(step)
        return pltpu.make_async_copy(acts_hbm.at[o], acts_raw.at[o], load_sems.at[step])

    for copy in load_small:
        copy.start()
    load_wide[0].start()
    load_acts(0).start()
    for copy in load_rest:
        copy.start()
    load_wide[1].start()

    barrier = pltpu.get_barrier_semaphore()
    for device in [pair_dev, x_dev, y_dev, xy_dev] + [z_dev(s) for s in range(last)]:
        pl.semaphore_signal(barrier, inc=1, device_id=device, device_id_type=MESH)

    def start_acts(step, carry):
        load_acts(step).start()
        return carry

    lax.fori_loop(1, outer, start_acts, 0)

    slots, tokens = token_ref.shape[1], grad_raw.shape[2]
    load_small[0].wait()
    load_small[1].wait()
    chosen = lax.broadcasted_iota(jnp.int32, (tokens, slots), 0) == token_ref[...]
    onehot = jnp.where(chosen, 1.0, 0.0).astype(jnp.bfloat16)
    live = lax.broadcasted_iota(jnp.int32, (1, slots), 1) < live_ref[0]
    weight = jnp.where(live, prob_ref[...], 0.0)

    def weigh(raw):
        picked = jnp.dot(raw, onehot, preferred_element_type=jnp.float32)
        return (picked * weight).astype(jnp.bfloat16)

    def copy_wide(i):
        g = grad_order[i]
        return remote(mine.at[g], peer.at[g], w_sems.at[0, i], w_sems.at[1, i], pair_dev)

    copy_rest = remote(
        mine_rest, peer_rest, w_sems.at[0, 2], w_sems.at[1, 2], pair_dev
    )

    def copy_acts(step):
        o = target(step)
        return remote(
            acts.at[1 - core, o], peer_acts.at[o],
            acts_sems.at[0, step], acts_sems.at[1, step], pair_dev,
        )

    def divide(step):
        o = target(step)
        load_acts(step).wait()
        for k in range(4):
            acts[k % 2, o, k // 2] = acts_raw[o, k * rows : (k + 1) * rows, :]

    load_wide[0].wait()
    mine[1 - half] = weigh(grad_raw[1 - half])
    pl.semaphore_wait(barrier, 4 + last)
    copy_wide(0).start()
    divide(0)
    copy_acts(0).start()
    for copy in load_rest:
        copy.wait()
    mine_rest[...] = weigh(rest_raw[...])
    copy_rest.start()
    load_wide[1].wait()
    mine[half] = weigh(grad_raw[half])
    copy_wide(1).start()

    def feed(step, carry):
        divide(step)
        copy_acts(step).start()
        return carry

    lax.fori_loop(1, outer, feed, 0)

    def contract(left, right):
        return lax.dot_general(
            left, right, (((1,), (1,)), ((), ())), preferred_element_type=jnp.float32
        )

    def term(step, a, b):
        o, m = target(step), b * (1 - core) + a * core
        column = a * (1 - core) + b * core
        return contract(acts[core, o, m], mine[column]) + contract(
            peer_acts[o, m], peer[column]
        )

    def rest_term(step):
        o = target(step)
        parts = [
            contract(mine_rest[...], acts[core, o, m])
            + contract(peer_rest[...], peer_acts[o, m])
            for m in range(2)
        ]
        return jnp.concatenate(parts, axis=1)

    def copy_a(step, k):
        return remote(
            send_a.at[step, k], recv_a.at[step, k],
            a_sems.at[0, step, k], a_sems.at[1, step, k], a_dev,
        )

    def copy_b(step):
        return remote(
            send_b.at[step], recv_b.at[step], b_sems.at[0, step], b_sems.at[1, step], b_dev
        )

    def copy_z(step):
        return remote(
            send_z.at[step], recv_z.at[step],
            z_sems.at[0, step], z_sems.at[1, step], z_dev(step),
        )

    def copy_r(step):
        return remote(
            send_r.at[step], recv_r.at[step],
            r_sems.at[0, step], r_sems.at[1, step], z_dev(step),
        )

    plane = (x_dev, y_dev, xy_dev)

    def copy_p(i):
        return remote(
            send_p.at[i], recv_p.at[i], p_sems.at[0, i], p_sems.at[1, i], plane[i]
        )

    def first(step, k):
        b = 1 - my_b if k == 0 else my_b
        send_a[step, k] = term(step, 1 - my_a, b).astype(jnp.bfloat16)
        copy_a(step, k).start()

    def rest_first(step):
        send_r[step] = rest_term(step).astype(jnp.bfloat16)
        copy_r(step).start()

    def second(step):
        total = term(step, my_a, 1 - my_b)
        copy_a(step, 0).wait_recv()
        total = total + recv_a[step, 0].astype(jnp.float32)
        send_b[step] = total.astype(jnp.bfloat16)
        copy_b(step).start()

    def third(step):
        total = term(step, my_a, my_b)
        copy_a(step, 1).wait_recv()
        total = total + recv_a[step, 1].astype(jnp.float32)
        copy_b(step).wait_recv()
        total = total + recv_b[step].astype(jnp.float32)
        send_z[step] = total.astype(jnp.bfloat16)
        copy_z(step).start()

    def rest_second():
        own_r[...] = rest_term(last)

        def add(step, carry):
            copy_r(step).wait_recv()
            own_r[...] += recv_r[step].astype(jnp.float32)
            return carry

        lax.fori_loop(0, last, add, 0)

        def piece(h):
            block = own_r[pl.ds(pl.multiple_of(h * rest, 16), rest), :]
            low, high = block[:, :rows], block[:, rows:]
            here = jnp.where(mid == 0, low, high)
            there = jnp.where(mid == 0, high, low)
            return here, there

        x_part, xy_part = piece(1 - half)
        mine_part, y_part = piece(half)
        for i, part in enumerate((x_part, y_part, xy_part)):
            send_p[i] = part.astype(jnp.bfloat16)
            copy_p(i).start()
        turned[...] = jnp.zeros_like(turned)
        turned[:rest, :rows] = mine_part

    def lead(step, both):
        copy_acts(step).wait_recv()
        first(step, 0)
        if both:
            copy_rest.wait_recv()

        @pl.when(step < last)
        def _():
            rest_first(step)

        if both:
            copy_wide(1).wait_recv()
        first(step, 1)

    copy_wide(0).wait_recv()
    lead(0, True)
    if outer > 1:
        lead(1, False)

    def stage(step, carry):
        @pl.when(step >= 1)
        def _():
            third(step - 1)

        second(step)

        @pl.when(step + 2 < outer)
        def _():
            lead(step + 2, False)

        @pl.when(step == min(1, last))
        def _():
            rest_second()

        return carry

    lax.fori_loop(0, outer, stage, 0)
    out_ref[:, :wide] = term(last, my_a, my_b)

    for i in range(3):
        copy_p(i).wait_recv()
        turned[:rest, :rows] += recv_p[i].astype(jnp.float32)
    out_ref[:, wide:] = turned[...].T[:rows, :rest]

    copy_a(last, 1).wait_recv()
    out_ref[:, :wide] += recv_a[last, 1].astype(jnp.float32)

    def add_z(step, carry):
        copy_z(step).wait_recv()
        out_ref[:, :wide] += recv_z[step].astype(jnp.float32)
        return carry

    lax.fori_loop(0, last, add_z, 0)
    copy_b(last).wait_recv()
    out_ref[:, :wide] += recv_b[last].astype(jnp.float32)

    def drain(step, carry):
        copy_acts(step).wait_send()
        copy_a(step, 0).wait_send()
        copy_a(step, 1).wait_send()
        copy_b(step).wait_send()
        return carry

    lax.fori_loop(0, outer, drain, 0)

    def drain_z(step, carry):
        copy_z(step).wait_send()
        copy_r(step).wait_send()
        return carry

    lax.fori_loop(0, last, drain_z, 0)
    copy_wide(0).wait_send()
    copy_wide(1).wait_send()
    copy_rest.wait_send()
    for i in range(3):
        copy_p(i).wait_send()


def shards(expert_act, grad_out, slot_token, slot_prob, live_count):
    slots, hidden = expert_act.shape
    tokens = grad_out.shape[0]
    ranks, halves = lax.axis_size("dp"), lax.axis_size("tensor")
    outer = ranks // 4
    rows, columns = hidden // ranks, grad_out.shape[1] // halves
    wide = columns // LANES * LANES
    rest = columns - wide
    scaling = 1.0 / math.sqrt(slots * ranks * halves)
    bf16, f32, dma = jnp.bfloat16, jnp.float32, pltpu.SemaphoreType.DMA
    anywhere = pl.BlockSpec(memory_space=pl.ANY)
    total = pl.pallas_call(
        functools.partial(kernel, outer, wide),
        out_shape=jax.ShapeDtypeStruct((rows, columns), f32),
        in_specs=[
            anywhere, anywhere, anywhere, anywhere,
            pl.BlockSpec(memory_space=pltpu.SMEM),
        ],
        out_specs=pl.BlockSpec(memory_space=pltpu.VMEM),
        scratch_shapes=[
            pltpu.VMEM((1, slots), jnp.int32),
            pltpu.VMEM((1, slots), f32),
            pltpu.VMEM((outer, 4 * rows, slots), bf16),
            pltpu.VMEM((halves, wide, tokens), bf16),
            pltpu.VMEM((halves * rest, tokens), bf16),
            pltpu.VMEM((2, outer, 2, rows, slots), bf16),
            pltpu.VMEM((outer, 2, rows, slots), bf16),
            pltpu.VMEM((halves, wide, slots), bf16),
            pltpu.VMEM((halves, wide, slots), bf16),
            pltpu.VMEM((halves * rest, slots), bf16),
            pltpu.VMEM((halves * rest, slots), bf16),
            pltpu.VMEM((outer, 2, rows, wide), bf16),
            pltpu.VMEM((outer, 2, rows, wide), bf16),
            pltpu.VMEM((outer, rows, wide), bf16),
            pltpu.VMEM((outer, rows, wide), bf16),
            pltpu.VMEM((outer - 1, rows, wide), bf16),
            pltpu.VMEM((outer - 1, rows, wide), bf16),
            pltpu.VMEM((outer - 1, halves * rest, 2 * rows), bf16),
            pltpu.VMEM((outer - 1, halves * rest, 2 * rows), bf16),
            pltpu.VMEM((halves * rest, 2 * rows), f32),
            pltpu.VMEM((3, rest, rows), bf16),
            pltpu.VMEM((3, rest, rows), bf16),
            pltpu.VMEM((pl.cdiv(rest, LANES) * LANES, pl.cdiv(rows, LANES) * LANES), f32),
            dma((2,)),
            dma((outer,)),
            dma((4,)),
            dma((2, outer)),
            dma((2, 3)),
            dma((2, outer, 2)),
            dma((2, outer)),
            dma((2, outer - 1)),
            dma((2, outer - 1)),
            dma((2, 3)),
        ],
        compiler_params=pltpu.CompilerParams(
            collective_id=0, has_side_effects=True, vmem_limit_bytes=53 * 2**20
        ),
    )(
        expert_act.T.reshape(outer, 4 * rows, slots),
        grad_out.T.reshape(halves, columns, tokens),
        slot_token[None, :],
        slot_prob[None, :],
        live_count,
    )
    return total * scaling


def solution(mesh):
    return jax.shard_map(
        shards,
        mesh=mesh,
        in_specs=(
            P(("dp", "tensor"), None),
            P(("dp", "tensor"), None),
            P(("dp", "tensor")),
            P(("dp", "tensor")),
            P(("dp", "tensor")),
        ),
        out_specs=P("dp", "tensor"),
        check_vma=False,
    )
```

time: 53.2 us -> 47.2 us (0.89)
  Pallas kernels: 50.1 us -> 44.2 us
    pallas_call x1, Pallas kernels: 50.1 us -> 44.2 us  [shards(): pl.pallas_call(functools.partial(kernel, outer, wide), out_shape=jax.Shap...]
where the time goes in v1:
time: 47.2 us; the launch traced here: 47 us
  Pallas kernels  44.2 us (94%)
  local copies, waits for them, and re-layouts  1.36 us (3%)
  other arithmetic  0.85 us (2%)
  between operations  0.67 us (1%)
    pallas_call x1, Pallas kernels, shards(): pl.pallas_call(functools.partial(kernel, outer, wide), out_shape=jax.Shap...  44.2 us
    unnamed x4, local copies, waits for them, and re-layouts  1.36 us

profile of v1, /device:TPU:0, one launch (start us, length us, event | category | flops | bytes accessed | tf_op | source)
XLA Modules:
  0.0 47.0 jit_solution(1211650986983196475)
XLA Ops:
  0.7 0.0 copy-start
  0.7 0.7 %copy-done = s32[512]{0:T(512)S(1)} copy-done((s32[512]{0:T(512)S(1)}, s32[512]{0:T(512)}, u32[]{:S(2)}) %copy-start) | copy-done | bytes 2072
  1.3 0.0 copy-start.1
  1.3 0.7 %copy-done.1 = f32[512]{0:T(512)S(1)} copy-done((f32[512]{0:T(512)S(1)}, f32[512]{0:T(512)}, u32[]{:S(2)}) %copy-start.1) | copy-done | bytes 2072
  2.0 44.2 %shard_map.55 = f32[180,720]{1,0:T(8,128)S(1)} custom-call(bf16[4,720,512]{2,1,0:T(8,128)(2,1)} %bitcast.10, bf16[2,720,1024]{2,1,0:T(8,128)(2,1)} %bitcast.11, s32[1,512]{1,0:T(1,128)S(1)} %bitcast.8, f32[1,512]{1,0:T(1,128)S(1)} %bitcast.9, s32[1]{0:T(128)S(6)} %copy.6.live_ref), custom_call_target="tpu_custom_call" | custom-call | tf_op jit(solution)/shard_map/pallas_call | solution.py:347
  46.2 0.8 %broadcast_multiply_fusion = f32[180,720]{1,0:T(8,128)} fusion(f32[180,720]{1,0:T(8,128)S(1)} %shard_map.55), kind=kLoop, calls=%fused_computation | loop fusion | flops 129600 | bytes 1036800 | tf_op jit(solution)/shard_map/mul | solution.py:400
Async XLA Ops:
  0.7 0.7 %copy-start = (s32[512]{0:T(512)S(1)}, s32[512]{0:T(512)}, u32[]{:S(2)}) copy-start(s32[512]{0:T(512)} %param.7) | copy-start | bytes 6148
  1.3 0.7 %copy-start.1 = (f32[512]{0:T(512)S(1)}, f32[512]{0:T(512)}, u32[]{:S(2)}) copy-start(f32[512]{0:T(512)} %param.8) | copy-start | bytes 6148

commit v2 on v0

v2 whole, which is shorter than its diff:
```python
import functools
import math

import jax
import jax.numpy as jnp
from jax import lax
from jax.experimental import pallas as pl
from jax.experimental.pallas import tpu as pltpu
from jax.sharding import PartitionSpec as P

MESH = pl.DeviceIdType.MESH
PIECE = 256


def kernel(
    outer, columns,
    acts_hbm, grad_hbm, token_hbm, prob_hbm, live_ref, out_ref,
    token_ref, prob_ref, acts_raw, grad_raw, acts, peer_acts, mine, peer,
    send_a, recv_a, send_b, recv_b, send_z, recv_z, send_r, recv_r,
    small_sems, load_sems, grad_sems, acts_sems, w_sems,
    a_sems, b_sems, z_sems, r_sems,
):
    dp = lax.axis_index("dp")
    half = lax.axis_index("tensor")
    core = lax.rem(dp, 2)
    mid = lax.rem(dp // 2, 2)
    own = dp // 4
    my_a = half * (1 - core) + mid * core
    my_b = mid * (1 - core) + half * core
    flip_mid = dp + 2 - 4 * mid
    pair_dev = {"dp": dp + 1 - 2 * core, "tensor": half}
    a_dev = {
        "dp": dp * (1 - core) + flip_mid * core,
        "tensor": (1 - half) * (1 - core) + half * core,
    }
    b_dev = {
        "dp": flip_mid * (1 - core) + dp * core,
        "tensor": half * (1 - core) + (1 - half) * core,
    }
    side = lax.rem(own, 2)
    near = own + 1 - 2 * side
    pieces, rows = mine.shape[1], acts.shape[3]
    far_total = (outer - 2) * pieces
    total_pieces = far_total + 1 + pieces
    raws = send_r.shape[0]
    spots = ((1 - my_a, 1 - my_b), (1 - my_a, my_b), (my_a, 1 - my_b), (my_a, my_b))

    def far(j):
        pair = lax.rem(own // 2 + 1 + j // 2, outer // 2)
        return 2 * pair + lax.rem(side + j, 2)

    def place(i):
        is_far, is_near = i < far_total, i == far_total
        o = jnp.where(is_far, far(jnp.minimum(i, far_total - 1) // pieces), own)
        o = jnp.where(is_near, near, o)
        p = jnp.where(is_far, lax.rem(i, pieces), i - far_total - 1)
        return o, jnp.where(is_near, pieces - 1, p)

    def z_dev(o):
        return {"dp": dp + (o - own) * 4, "tensor": half}

    def remote(src, dst, sems, device):
        return pltpu.make_async_remote_copy(
            src_ref=src, dst_ref=dst, send_sem=sems[0], recv_sem=sems[1],
            device_id=device, device_id_type=MESH,
        )

    grad_order = (1 - half, half)
    act_order = [far(0), near] + [far(j) for j in range(1, outer - 2)] + [own]

    load_small = [
        pltpu.make_async_copy(token_hbm, token_ref, small_sems.at[0]),
        pltpu.make_async_copy(prob_hbm, prob_ref, small_sems.at[1]),
    ]

    def load_grad(p, i):
        window = pl.ds(p * PIECE, min(PIECE, columns - p * PIECE))
        g = grad_order[i]
        return pltpu.make_async_copy(
            grad_hbm.at[g, window], grad_raw.at[g, window], grad_sems.at[p, i]
        )

    def load_acts(o):
        return pltpu.make_async_copy(acts_hbm.at[o], acts_raw.at[o], load_sems.at[o])

    for copy in load_small:
        copy.start()
    load_grad(0, 0).start()
    load_acts(act_order[0]).start()
    load_grad(0, 1).start()
    load_acts(act_order[1]).start()
    for p in range(1, pieces):
        for i in range(2):
            load_grad(p, i).start()
    for o in act_order[2:]:
        load_acts(o).start()

    barrier = pltpu.get_barrier_semaphore()
    others = act_order[:-1]
    for device in [pair_dev, a_dev, b_dev] + [z_dev(o) for o in others]:
        pl.semaphore_signal(barrier, inc=1, device_id=device, device_id_type=MESH)

    slots, tokens = token_ref.shape[1], grad_raw.shape[2]
    if pieces * PIECE > columns:
        spare = pieces * PIECE - columns
        grad_raw[:, columns:] = jnp.zeros((2, spare, tokens), grad_raw.dtype)
    load_small[0].wait()
    load_small[1].wait()
    chosen = lax.broadcasted_iota(jnp.int32, (tokens, slots), 0) == token_ref[...]
    onehot = jnp.where(chosen, 1.0, 0.0).astype(jnp.bfloat16)
    live = lax.broadcasted_iota(jnp.int32, (1, slots), 1) < live_ref[0]
    weight = jnp.where(live, prob_ref[...], 0.0)

    def copy_w(p, i):
        g = grad_order[i]
        return remote(
            mine.at[g, p], peer.at[g, p],
            (w_sems.at[0, p, i], w_sems.at[1, p, i]), pair_dev,
        )

    def copy_acts(o):
        return remote(
            acts.at[1 - core, o], peer_acts.at[o],
            (acts_sems.at[0, o], acts_sems.at[1, o]), pair_dev,
        )

    def weigh(p, i):
        g = grad_order[i]
        load_grad(p, i).wait()
        picked = jnp.dot(
            grad_raw[g, p * PIECE : (p + 1) * PIECE], onehot,
            preferred_element_type=jnp.float32,
        )
        mine[g, p] = (picked * weight).astype(jnp.bfloat16)

    def divide(o):
        load_acts(o).wait()
        for k in range(4):
            acts[k % 2, o, k // 2] = acts_raw[o, k * rows : (k + 1) * rows, :]

    def contract(left, right):
        return lax.dot_general(
            left, right, (((1,), (1,)), ((), ())), preferred_element_type=jnp.float32
        )

    def term(o, p, spot):
        a, b = spot
        m = b * (1 - core) + a * core
        column = a * (1 - core) + b * core
        return contract(acts[core, o, m], mine[column, p]) + contract(
            peer_acts[o, m], peer[column, p]
        )

    def copy_a(i, k):
        return remote(
            send_a.at[i, k], recv_a.at[i, k],
            (a_sems.at[0, i, k], a_sems.at[1, i, k]), a_dev,
        )

    def copy_b(i):
        return remote(send_b.at[i], recv_b.at[i], (b_sems.at[0, i], b_sems.at[1, i]), b_dev)

    def copy_z(i):
        return remote(
            send_z.at[i], recv_z.at[i], (z_sems.at[0, i], z_sems.at[1, i]),
            z_dev(place(i)[0]),
        )

    def copy_r(r):
        return remote(
            send_r.at[r], recv_r.at[r], (r_sems.at[0, r], r_sems.at[1, r]), z_dev(near)
        )

    def with_raw(i, q, put, total):
        put(total)

        @pl.when((i > far_total) & (i < total_pieces - 1))
        def _():
            r = (i - far_total - 1) * 4 + q
            copy_r(r).wait_recv()
            put(total + recv_r[r].astype(jnp.float32))

    def first(i):
        o, p = place(i)
        for k in range(2):

            def put(total):
                send_a[i, k] = total.astype(jnp.bfloat16)

            with_raw(i, k, put, term(o, p, spots[k]))
            copy_a(i, k).start()

    def second(i):
        o, p = place(i)
        total = term(o, p, spots[2])
        copy_a(i, 0).wait_recv()

        def put(total):
            send_b[i] = total.astype(jnp.bfloat16)

        with_raw(i, 2, put, total + recv_a[i, 0].astype(jnp.float32))
        copy_b(i).start()

    def third(i):
        o, p = place(i)
        total = term(o, p, spots[3])
        copy_a(i, 1).wait_recv()
        total = total + recv_a[i, 1].astype(jnp.float32)
        copy_b(i).wait_recv()
        total = total + recv_b[i].astype(jnp.float32)
        send_z[i] = total.astype(jnp.bfloat16)
        copy_z(i).start()

    def raw(r):
        q = lax.rem(r, 4)
        a = jnp.where(q < 2, 1 - my_a, my_a)
        b = jnp.where(lax.rem(q, 2) == 0, 1 - my_b, my_b)
        send_r[r] = term(near, r // 4, (a, b)).astype(jnp.bfloat16)
        copy_r(r).start()

    weigh(0, 0)
    divide(act_order[0])
    pl.semaphore_wait(barrier, 2 + outer)
    copy_acts(act_order[0]).start()
    copy_w(0, 0).start()
    weigh(0, 1)
    copy_w(0, 1).start()
    divide(act_order[1])
    copy_acts(act_order[1]).start()
    for i in range(2):
        weigh(1, i)
        copy_w(1, i).start()
    copy_acts(act_order[0]).wait_recv()
    copy_w(0, 0).wait_recv()
    copy_w(0, 1).wait_recv()
    first(0)
    copy_acts(act_order[1]).wait_recv()
    raw(0)
    raw(1)
    for p in range(2, pieces):
        for i in range(2):
            weigh(p, i)
            copy_w(p, i).start()
    for o in act_order[2:]:
        divide(o)
        copy_acts(o).start()
    copy_w(1, 0).wait_recv()
    copy_w(1, 1).wait_recv()
    first(1)
    raw(2)
    for p in range(2, pieces):
        for i in range(2):
            copy_w(p, i).wait_recv()
    for o in act_order[2:]:
        copy_acts(o).wait_recv()

    def stage(i, carry):
        second(i)

        @pl.when(i + 2 < total_pieces)
        def _():
            first(i + 2)

        @pl.when(i + 3 < raws)
        def _():
            raw(i + 3)

        @pl.when((i >= 1) & (i - 1 <= far_total))
        def _():
            third(i - 1)

        return carry

    lax.fori_loop(0, total_pieces, stage, 0)

    for p in range(pieces):
        i = far_total + 1 + p
        width = min(PIECE, columns - p * PIECE)
        total = term(own, p, spots[3])
        if p < pieces - 1:
            copy_r(p * 4 + 3).wait_recv()
            total = total + recv_r[p * 4 + 3].astype(jnp.float32)
        copy_a(i, 1).wait_recv()
        total = total + recv_a[i, 1].astype(jnp.float32)
        for j in range(outer - 2):
            copy_z(j * pieces + p).wait_recv()
            total = total + recv_z[j * pieces + p].astype(jnp.float32)
        copy_b(i).wait_recv()
        total = total + recv_b[i].astype(jnp.float32)
        if p == pieces - 1:
            copy_z(far_total).wait_recv()
            total = total + recv_z[far_total].astype(jnp.float32)
        out_ref[:, p * PIECE : p * PIECE + width] = total[:, :width]

    def drain(i, carry):
        copy_a(i, 0).wait_send()
        copy_a(i, 1).wait_send()
        copy_b(i).wait_send()
        return carry

    lax.fori_loop(0, total_pieces, drain, 0)

    def drain_z(i, carry):
        copy_z(i).wait_send()
        return carry

    lax.fori_loop(0, far_total + 1, drain_z, 0)

    def drain_r(r, carry):
        copy_r(r).wait_send()
        return carry

    lax.fori_loop(0, raws, drain_r, 0)
    for p in range(pieces):
        for i in range(2):
            copy_w(p, i).wait_send()
    for o in act_order:
        copy_acts(o).wait_send()


def shards(expert_act, grad_out, slot_token, slot_prob, live_count):
    slots, hidden = expert_act.shape
    tokens = grad_out.shape[0]
    ranks, halves = lax.axis_size("dp"), lax.axis_size("tensor")
    outer = ranks // 4
    rows, columns = hidden // ranks, grad_out.shape[1] // halves
    pieces = pl.cdiv(columns, PIECE)
    count = (outer - 1) * pieces + 1
    raws = 4 * (pieces - 1)
    scaling = 1.0 / math.sqrt(slots * ranks * halves)
    bf16, f32, dma = jnp.bfloat16, jnp.float32, pltpu.SemaphoreType.DMA
    anywhere = pl.BlockSpec(memory_space=pl.ANY)
    total = pl.pallas_call(
        functools.partial(kernel, outer, columns),
        out_shape=jax.ShapeDtypeStruct((rows, columns), f32),
        in_specs=[
            anywhere, anywhere, anywhere, anywhere,
            pl.BlockSpec(memory_space=pltpu.SMEM),
        ],
        out_specs=pl.BlockSpec(memory_space=pltpu.VMEM),
        scratch_shapes=[
            pltpu.VMEM((1, slots), jnp.int32),
            pltpu.VMEM((1, slots), f32),
            pltpu.VMEM((outer, 4 * rows, slots), bf16),
            pltpu.VMEM((halves, pieces * PIECE, tokens), bf16),
            pltpu.VMEM((2, outer, 2, rows, slots), bf16),
            pltpu.VMEM((outer, 2, rows, slots), bf16),
            pltpu.VMEM((halves, pieces, PIECE, slots), bf16),
            pltpu.VMEM((halves, pieces, PIECE, slots), bf16),
            pltpu.VMEM((count, 2, rows, PIECE), bf16),
            pltpu.VMEM((count, 2, rows, PIECE), bf16),
            pltpu.VMEM((count, rows, PIECE), bf16),
            pltpu.VMEM((count, rows, PIECE), bf16),
            pltpu.VMEM((count - pieces, rows, PIECE), bf16),
            pltpu.VMEM((count - pieces, rows, PIECE), bf16),
            pltpu.VMEM((raws, rows, PIECE), bf16),
            pltpu.VMEM((raws, rows, PIECE), bf16),
            dma((2,)),
            dma((outer,)),
            dma((pieces, 2)),
            dma((2, outer)),
            dma((2, pieces, 2)),
            dma((2, count, 2)),
            dma((2, count)),
            dma((2, count - pieces)),
            dma((2, raws)),
        ],
        compiler_params=pltpu.CompilerParams(
            collective_id=0, has_side_effects=True, vmem_limit_bytes=53 * 2**20
        ),
    )(
        expert_act.T.reshape(outer, 4 * rows, slots),
        grad_out.T.reshape(halves, columns, tokens),
        slot_token[None, :],
        slot_prob[None, :],
        live_count,
    )
    return total * scaling


def solution(mesh):
    return jax.shard_map(
        shards,
        mesh=mesh,
        in_specs=(
            P(("dp", "tensor"), None),
            P(("dp", "tensor"), None),
            P(("dp", "tensor")),
            P(("dp", "tensor")),
            P(("dp", "tensor")),
        ),
        out_specs=P("dp", "tensor"),
        check_vma=False,
    )
```

time: 53.2 us -> 47.7 us (0.90)
  Pallas kernels: 50.1 us -> 44.6 us
    pallas_call x1, Pallas kernels: 50.1 us -> 44.6 us  [shards(): pl.pallas_call(functools.partial(kernel, outer, columns), out_shape=jax.S...]
where the time goes in v2:
time: 47.7 us; the launch traced here: 47.5 us
  Pallas kernels  44.6 us (94%)
  local copies, waits for them, and re-layouts  1.36 us (3%)
  other arithmetic  0.85 us (2%)
  between operations  0.67 us (1%)
    pallas_call x1, Pallas kernels, shards(): pl.pallas_call(functools.partial(kernel, outer, columns), out_shape=jax.S...  44.6 us
    unnamed x4, local copies, waits for them, and re-layouts  1.36 us

profile of v2, /device:TPU:0, one launch (start us, length us, event | category | flops | bytes accessed | tf_op | source)
XLA Modules:
  0.0 47.5 jit_solution(3095821787071600575)
XLA Ops:
  0.7 0.0 copy-start
  0.7 0.7 %copy-done = s32[512]{0:T(512)S(1)} copy-done((s32[512]{0:T(512)S(1)}, s32[512]{0:T(512)}, u32[]{:S(2)}) %copy-start) | copy-done | bytes 2072
  1.3 0.0 copy-start.1
  1.3 0.7 %copy-done.1 = f32[512]{0:T(512)S(1)} copy-done((f32[512]{0:T(512)S(1)}, f32[512]{0:T(512)}, u32[]{:S(2)}) %copy-start.1) | copy-done | bytes 2072
  2.0 44.6 %shard_map.55 = f32[180,720]{1,0:T(8,128)S(1)} custom-call(bf16[4,720,512]{2,1,0:T(8,128)(2,1)} %bitcast.10, bf16[2,720,1024]{2,1,0:T(8,128)(2,1)} %bitcast.11, s32[1,512]{1,0:T(1,128)S(1)} %bitcast.8, f32[1,512]{1,0:T(1,128)S(1)} %bitcast.9, s32[1]{0:T(128)S(6)} %copy.6.live_ref), custom_call_target="tpu_custom_call" | custom-call | tf_op jit(solution)/shard_map/pallas_call | solution.py:333
  46.6 0.8 %broadcast_multiply_fusion = f32[180,720]{1,0:T(8,128)} fusion(f32[180,720]{1,0:T(8,128)S(1)} %shard_map.55), kind=kLoop, calls=%fused_computation | loop fusion | flops 129600 | bytes 1036800 | tf_op jit(solution)/shard_map/mul | solution.py:378
Async XLA Ops:
  0.7 0.7 %copy-start = (s32[512]{0:T(512)S(1)}, s32[512]{0:T(512)}, u32[]{:S(2)}) copy-start(s32[512]{0:T(512)} %param.7) | copy-start | bytes 6148
  1.3 0.7 %copy-start.1 = (f32[512]{0:T(512)S(1)}, f32[512]{0:T(512)}, u32[]{:S(2)}) copy-start(f32[512]{0:T(512)} %param.8) | copy-start | bytes 6148

commit v3 on v2

v3 whole, which is shorter than its diff:
```python
import functools
import math

import jax
import jax.numpy as jnp
from jax import lax
from jax.experimental import pallas as pl
from jax.experimental.pallas import tpu as pltpu
from jax.sharding import PartitionSpec as P

MESH = pl.DeviceIdType.MESH
PIECE = 256
LANES = 128


TUNED = (2, 3)
ORDER = (
    "F000", "X000", "G00", "N0", "R0", "X010", "X020", "F01", "X001",
    "H02", "S00", "X011", "N1", "S01", "R1", "H03", "X021", "F10",
    "S02", "F11", "H12", "T00", "X100", "H13", "N2", "X110", "N3",
    "T01", "F30", "X120", "H32", "T02", "X101", "R2", "F31", "S10",
    "X111", "H33", "S11", "X121", "S12", "Y00", "X220", "T10", "Y01",
    "X221", "T11", "X300", "Y02", "X310", "T12", "R3", "S22", "X320",
    "Y10", "X301", "S30", "X311", "T22", "Y11", "S31", "X321", "Y12",
    "S32",
)


def plan(fars, pieces):
    if (fars, pieces) == TUNED:
        return [(token[0], *map(int, token[1:])) for token in ORDER]
    near, own, every = fars, fars + 1, range(pieces)
    steps = [("F", 0, 0, p) for p in every] + [("F", 0, 1, p) for p in every]
    steps += [("X", 0, p, k) for k in range(2) for p in every]
    steps += [(name, q) for q in range(4) for name in "NR"]
    steps += [("X", near, pieces - 1, k) for k in range(2)]
    for j in list(range(fars)) + [near, own]:
        then = j + 1 if j + 1 < fars else own
        if j < near:
            steps += [("F", then, k, p) for k in range(2) for p in every]
            steps += [("H", j, 2), ("H", j, 3)]
        if j == own:
            steps += [("H", j, 2), ("H", j, 3)]
        mine = [pieces - 1] if j == near else every
        steps += [("S", j, p) for p in mine]
        if j < near:
            steps += [("X", then, p, k) for k in range(2) for p in every]
        if j < own:
            steps += [("T", j, p) for p in mine]
        if j < near:
            steps += [("Y", j, p) for p in every]
    return steps


def kernel(
    outer,
    acts_hbm, grad_hbm, token_ref, prob_ref, live_ref, out_ref,
    acts_raw, grad_raw, acts, peer_acts, mine, peer, onehot, weight, held,
    send_a, recv_a, send_b, recv_b, send_z, recv_z, recv_y, send_r, recv_r,
    load_sems, grad_sems, acts_sems, w_sems,
    a_sems, b_sems, z_sems, y_sems, r_sems,
):
    dp = lax.axis_index("dp")
    half = lax.axis_index("tensor")
    core = lax.rem(dp, 2)
    mid = lax.rem(dp // 2, 2)
    own = dp // 4
    my_a = half * (1 - core) + mid * core
    my_b = mid * (1 - core) + half * core
    flip_mid = dp + 2 - 4 * mid
    pair_dev = {"dp": dp + 1 - 2 * core, "tensor": half}
    a_dev = {
        "dp": dp * (1 - core) + flip_mid * core,
        "tensor": (1 - half) * (1 - core) + half * core,
    }
    b_dev = {
        "dp": flip_mid * (1 - core) + dp * core,
        "tensor": half * (1 - core) + (1 - half) * core,
    }
    side = lax.rem(own, 2)
    near = own + 1 - 2 * side
    columns, pieces = out_ref.shape[1], mine.shape[2] // PIECE
    rows, slots = acts.shape[3], acts.shape[4]
    tokens = grad_raw.shape[2]
    fars = outer - 2
    far_total = fars * pieces
    raws = send_r.shape[0]
    spots = ((1 - my_a, 1 - my_b), (1 - my_a, my_b), (my_a, 1 - my_b), (my_a, my_b))

    def far_pair(j):
        pair = lax.rem(own // 2 + 1 + j // 2, outer // 2)
        return pair, jnp.where(pair > own // 2, 1, 0)

    def far(j):
        pair, up = far_pair(j)
        return 2 * pair + (up if j % 2 == 0 else 1 - up)

    def leads(j):
        return side == far_pair(j)[1]

    targets = [far(j) for j in range(fars)] + [near, own]
    NEAR, OWN = fars, fars + 1

    def z_dev(o):
        return {"dp": dp + (o - own) * 4, "tensor": half}

    def remote(src, dst, sems, device):
        return pltpu.make_async_remote_copy(
            src_ref=src, dst_ref=dst, send_sem=sems[0], recv_sem=sems[1],
            device_id=device, device_id_type=MESH,
        )

    grad_order = (1 - half, half)

    def load_grad(i, j):
        g = grad_order[i]
        window = pl.ds(0, PIECE) if j == 0 else pl.ds(PIECE, columns - PIECE)
        return pltpu.make_async_copy(
            grad_hbm.at[g, window], grad_raw.at[g, window], grad_sems.at[i, j]
        )

    def load_acts(step):
        o = targets[step]
        return pltpu.make_async_copy(acts_hbm.at[o], acts_raw.at[o], load_sems.at[step])

    act_order = [0, NEAR] + list(range(1, fars)) + [OWN]
    load_grad(0, 0).start()
    load_acts(act_order[0]).start()
    load_grad(0, 1).start()
    load_acts(act_order[1]).start()
    for j in range(2):
        load_grad(1, j).start()
    for step in act_order[2:]:
        load_acts(step).start()

    barrier = pltpu.get_barrier_semaphore()
    for device in [pair_dev, a_dev, b_dev] + [z_dev(o) for o in targets[:OWN]]:
        pl.semaphore_signal(barrier, inc=1, device_id=device, device_id_type=MESH)

    def turn(row):
        return jnp.broadcast_to(row.astype(jnp.float32), (LANES, slots)).T

    token = turn(token_ref[...])
    lane = lax.broadcasted_iota(jnp.int32, (slots, LANES), 1).astype(jnp.float32)
    for t in range(0, tokens, LANES):
        onehot[:, t : t + LANES] = jnp.where(token - t == lane, 1.0, 0.0).astype(
            onehot.dtype
        )
    live = lax.broadcasted_iota(jnp.int32, (1, slots), 1) < live_ref[0]
    weight[...] = turn(jnp.where(live, prob_ref[...], 0.0))
    if pieces * PIECE > columns:
        ragged = columns // LANES * LANES
        mine[:, :, ragged:] = jnp.zeros(
            (2, slots, pieces * PIECE - ragged), mine.dtype
        )

    def span(p):
        return slice(p * PIECE, (p + 1) * PIECE)

    def copy_w(i, p):
        g = grad_order[i]
        return remote(
            mine.at[g, :, pl.ds(p * PIECE, PIECE)],
            peer.at[g, :, pl.ds(p * PIECE, PIECE)],
            (w_sems.at[0, i, p], w_sems.at[1, i, p]), pair_dev,
        )

    def copy_acts(step):
        o = targets[step]
        return remote(
            acts.at[1 - core, o], peer_acts.at[o],
            (acts_sems.at[0, step], acts_sems.at[1, step]), pair_dev,
        )

    def weigh(i, begin, end):
        g = grad_order[i]
        picked = lax.dot_general(
            onehot[...], grad_raw[g, begin:end], (((1,), (1,)), ((), ())),
            preferred_element_type=jnp.float32,
        )
        for t in range(begin, end, LANES):
            stop = min(t + LANES, end)
            mine[g, :, t:stop] = (
                picked[:, t - begin : stop - begin] * weight[:, : stop - t]
            ).astype(jnp.bfloat16)

    def divide(step):
        o = targets[step]
        load_acts(step).wait()
        for k in range(4):
            acts[k % 2, o, k // 2] = acts_raw[o, k * rows : (k + 1) * rows, :]

    def contract(left, right):
        return jnp.dot(left, right, preferred_element_type=jnp.float32)

    def term(step, q, window=slice(None)):
        o = targets[step]
        a, b = spots[q]
        m = b * (1 - core) + a * core
        column = a * (1 - core) + b * core
        return contract(acts[core, o, m], mine[column, :, window]) + contract(
            peer_acts[o, m], peer[column, :, window]
        )

    def index(step, p):
        return step * pieces + p if step < NEAR else far_total + (0 if step == NEAR else 1 + p)

    def copy_a(step, p, k):
        i = index(step, p)
        return remote(
            send_a.at[i, k], recv_a.at[i, k],
            (a_sems.at[0, i, k], a_sems.at[1, i, k]), a_dev,
        )

    def copy_b(step, p):
        i = index(step, p)
        return remote(send_b.at[i], recv_b.at[i], (b_sems.at[0, i], b_sems.at[1, i]), b_dev)

    def slot(step, p):
        return step // 2 * pieces + p if step < NEAR else fars // 2 * pieces

    def copy_z(step, p):
        i, j = index(step, p), slot(step, p)
        return remote(
            send_z.at[i], recv_z.at[j], (z_sems.at[0, i], z_sems.at[1, j]),
            z_dev(targets[step]),
        )

    def copy_y(step, p):
        i = index(step, p)
        return remote(
            send_z.at[i], recv_y.at[i], (z_sems.at[0, i], y_sems.at[i]), z_dev(near)
        )

    def copy_r(r):
        return remote(
            send_r.at[r], recv_r.at[r], (r_sems.at[0, r], r_sems.at[1, r]), z_dev(near)
        )

    def raw_in(p, q):
        r = p * 4 + q
        copy_r(r).wait_recv()
        return recv_r[r].astype(jnp.float32)

    def wide(ref):
        return ref[...].astype(jnp.float32)

    seen = set()

    def need(step, q, pieces_end):
        wanted = [copy_acts(step)] if ("acts", step) not in seen else []
        seen.add(("acts", step))
        for i in range(1 if q == 0 else 2):
            for p in range(pieces_end):
                if (i, p) not in seen:
                    seen.add((i, p))
                    wanted.append(copy_w(i, p))
        for copy in wanted:
            copy.wait_recv()

    def first(step, k, p=None):
        begin, end = (0, pieces) if p is None else (p, p + 1)
        need(step, k, end)
        total = term(step, k, slice(begin * PIECE, end * PIECE))
        for p in range(begin, end):
            part = total[:, span(p - begin)]
            if step == OWN and p < pieces - 1:
                part = part + raw_in(p, k)
            send_a[index(step, p), k] = part.astype(jnp.bfloat16)

    def first_rest(step, k):
        need(step, k, pieces)
        total = term(step, k, slice(PIECE, pieces * PIECE))
        for p in range(1, pieces):
            send_a[index(step, p), k] = total[:, span(p - 1)].astype(jnp.bfloat16)

    def send_first(step, p, k):
        copy_a(step, p, k).start()

    def near_all(q):
        need(NEAR, q, pieces)
        total = term(NEAR, q)
        for p in range(pieces - 1):
            send_r[p * 4 + q] = total[:, span(p)].astype(jnp.bfloat16)
        p = pieces - 1
        part = total[:, span(p)]
        if q < 2:
            send_a[index(NEAR, p), q] = part.astype(jnp.bfloat16)
        else:
            held[NEAR, q - 2, :, span(p)] = part

    def send_raw(q):
        for p in range(pieces - 1):
            copy_r(p * 4 + q).start()

    def hold(step, q):
        need(step, q, pieces)
        held[step, q - 2] = term(step, q)

    def second(step, p):
        copy_a(step, p, 0).wait_recv()
        total = held[step, 0, :, span(p)] + wide(recv_a.at[index(step, p), 0])
        if step == OWN and p < pieces - 1:
            total = total + raw_in(p, 2)
        send_b[index(step, p)] = total.astype(jnp.bfloat16)
        copy_b(step, p).start()

    def third(step, p):
        copy_a(step, p, 1).wait_recv()
        copy_b(step, p).wait_recv()
        i = index(step, p)
        total = held[step, 1, :, span(p)] + wide(recv_a.at[i, 1]) + wide(recv_b.at[i])
        if step == NEAR:
            send_z[i] = total.astype(jnp.bfloat16)
            copy_z(step, p).start()
            return

        @pl.when(leads(step))
        def _():
            held[step, 1, :, span(p)] = total

        @pl.when(jnp.logical_not(leads(step)))
        def _():
            send_z[i] = total.astype(jnp.bfloat16)
            copy_y(step, p).start()

    def forward(step, p):
        i = index(step, p)

        @pl.when(leads(step))
        def _():
            copy_y(step, p).wait_recv()
            total = held[step, 1, :, span(p)] + wide(recv_y.at[i])
            send_z[i] = total.astype(jnp.bfloat16)
            copy_z(step, p).start()

    load_grad(0, 0).wait()
    weigh(0, 0, PIECE)
    divide(act_order[0])
    pl.semaphore_wait(barrier, 2 + outer)
    copy_acts(act_order[0]).start()
    copy_w(0, 0).start()
    load_grad(0, 1).wait()
    weigh(0, PIECE, columns)
    for p in range(1, pieces):
        copy_w(0, p).start()
    divide(NEAR)
    copy_acts(NEAR).start()
    for j in range(2):
        load_grad(1, j).wait()
    weigh(1, 0, columns)
    for p in range(pieces):
        copy_w(1, p).start()
    for step in act_order[2:]:
        divide(step)
        copy_acts(step).start()
    actions = {
        "F": first, "G": first_rest, "X": send_first, "N": near_all, "R": send_raw,
        "H": hold, "S": second, "T": third, "Y": forward,
    }
    for name, *where in plan(fars, pieces):
        actions[name](*where)

    for step in range(outer):
        for p in range(pieces):
            if step == NEAR and p < pieces - 1:
                continue
            copy_a(step, p, 0).wait_send()
            copy_a(step, p, 1).wait_send()
            if step < NEAR:
                copy_b(step, p).wait_send()
        copy_acts(step).wait_send()
    for r in range(raws):
        copy_r(r).wait_send()
    for i in range(2):
        for p in range(pieces):
            copy_w(i, p).wait_send()

    for p in range(pieces):
        i = index(OWN, p)
        width = min(PIECE, columns - p * PIECE)
        total = held[OWN, 1, :, span(p)]
        if p < pieces - 1:
            total = total + raw_in(p, 3)
        copy_a(OWN, p, 1).wait_recv()
        total = total + wide(recv_a.at[i, 1])
        held[OWN, 1, :, span(p)] = total
    for p in range(pieces):
        i = index(OWN, p)
        width = min(PIECE, columns - p * PIECE)
        copy_b(OWN, p).wait_recv()
        total = held[OWN, 1, :, span(p)] + wide(recv_b.at[i])
        for step in range(0, fars, 2):
            copy_z(step, p).wait_recv()
            total = total + wide(recv_z.at[slot(step, p)])
        if p == pieces - 1:
            copy_z(NEAR, p).wait_recv()
            total = total + wide(recv_z.at[slot(NEAR, p)])
        out_ref[:, p * PIECE : p * PIECE + width] = total[:, :width]
        copy_b(OWN, p).wait_send()
    for step in range(fars):
        for p in range(pieces):
            copy_z(step, p).wait_send()
    copy_b(NEAR, pieces - 1).wait_send()
    copy_z(NEAR, pieces - 1).wait_send()


def shards(expert_act, grad_out, slot_token, slot_prob, live_count):
    slots, hidden = expert_act.shape
    tokens = grad_out.shape[0]
    ranks, halves = lax.axis_size("dp"), lax.axis_size("tensor")
    outer = ranks // 4
    rows, columns = hidden // ranks, grad_out.shape[1] // halves
    pieces = pl.cdiv(columns, PIECE)
    count = (outer - 1) * pieces + 1
    raws = 4 * (pieces - 1)
    scaling = 1.0 / math.sqrt(slots * ranks * halves)
    bf16, f32, dma = jnp.bfloat16, jnp.float32, pltpu.SemaphoreType.DMA
    anywhere = pl.BlockSpec(memory_space=pl.ANY)
    total = pl.pallas_call(
        functools.partial(kernel, outer),
        out_shape=jax.ShapeDtypeStruct((rows, columns), f32),
        in_specs=[
            anywhere,
            anywhere,
            pl.BlockSpec(memory_space=pltpu.VMEM),
            pl.BlockSpec(memory_space=pltpu.VMEM),
            pl.BlockSpec(memory_space=pltpu.SMEM),
        ],
        out_specs=pl.BlockSpec(memory_space=pltpu.VMEM),
        scratch_shapes=[
            pltpu.VMEM((outer, 4 * rows, slots), bf16),
            pltpu.VMEM((halves, columns, tokens), bf16),
            pltpu.VMEM((2, outer, 2, rows, slots), bf16),
            pltpu.VMEM((outer, 2, rows, slots), bf16),
            pltpu.VMEM((halves, slots, pieces * PIECE), bf16),
            pltpu.VMEM((halves, slots, pieces * PIECE), bf16),
            pltpu.VMEM((slots, tokens), bf16),
            pltpu.VMEM((slots, LANES), f32),
            pltpu.VMEM((outer, 2, rows, pieces * PIECE), f32),
            pltpu.VMEM((count, 2, rows, PIECE), bf16),
            pltpu.VMEM((count, 2, rows, PIECE), bf16),
            pltpu.VMEM((count, rows, PIECE), bf16),
            pltpu.VMEM((count, rows, PIECE), bf16),
            pltpu.VMEM((count - pieces, rows, PIECE), bf16),
            pltpu.VMEM((count - pieces, rows, PIECE), bf16),
            pltpu.VMEM((count - pieces, rows, PIECE), bf16),
            pltpu.VMEM((raws, rows, PIECE), bf16),
            pltpu.VMEM((raws, rows, PIECE), bf16),
            dma((outer,)),
            dma((2, 2)),
            dma((2, outer)),
            dma((2, 2, pieces)),
            dma((2, count, 2)),
            dma((2, count)),
            dma((2, count - pieces)),
            dma((count - pieces,)),
            dma((2, raws)),
        ],
        compiler_params=pltpu.CompilerParams(
            collective_id=0, has_side_effects=True, vmem_limit_bytes=53 * 2**20
        ),
    )(
        expert_act.T.reshape(outer, 4 * rows, slots),
        grad_out.T.reshape(halves, columns, tokens),
        slot_token[None, :],
        slot_prob[None, :],
        live_count,
    )
    return total * scaling


def solution(mesh):
    return jax.shard_map(
        shards,
        mesh=mesh,
        in_specs=(
            P(("dp", "tensor"), None),
            P(("dp", "tensor"), None),
            P(("dp", "tensor")),
            P(("dp", "tensor")),
            P(("dp", "tensor")),
        ),
        out_specs=P("dp", "tensor"),
        check_vma=False,
    )
```

time: 47.7 us -> 45.6 us (0.956)
  Pallas kernels: 44.6 us -> 42.6 us
    pallas_call x1, Pallas kernels: 44.6 us -> 42.6 us  [shards(): pl.pallas_call(functools.partial(kernel, outer), out_shape=jax.ShapeDtype...]
where the time goes in v3:
time: 45.6 us; the launch traced here: 45.5 us
  Pallas kernels  42.6 us (93%)
  local copies, waits for them, and re-layouts  1.36 us (3%)
  other arithmetic  0.85 us (2%)
  between operations  0.67 us (1%)
    pallas_call x1, Pallas kernels, shards(): pl.pallas_call(functools.partial(kernel, outer), out_shape=jax.ShapeDtype...  42.6 us
    unnamed x4, local copies, waits for them, and re-layouts  1.36 us

profile of v3, /device:TPU:0, one launch (start us, length us, event | category | flops | bytes accessed | tf_op | source)
XLA Modules:
  0.0 45.5 jit_solution(6890536925268607774)
XLA Ops:
  0.7 0.0 copy-start
  0.7 0.7 %copy-done = s32[512]{0:T(512)S(1)} copy-done((s32[512]{0:T(512)S(1)}, s32[512]{0:T(512)}, u32[]{:S(2)}) %copy-start) | copy-done | bytes 2072
  1.3 0.0 copy-start.1
  1.3 0.7 %copy-done.1 = f32[512]{0:T(512)S(1)} copy-done((f32[512]{0:T(512)S(1)}, f32[512]{0:T(512)}, u32[]{:S(2)}) %copy-start.1) | copy-done | bytes 2072
  2.0 42.6 %shard_map.55 = f32[180,720]{1,0:T(8,128)S(1)} custom-call(bf16[4,720,512]{2,1,0:T(8,128)(2,1)} %bitcast.10, bf16[2,720,1024]{2,1,0:T(8,128)(2,1)} %bitcast.11, s32[1,512]{1,0:T(1,128)S(1)} %bitcast.8, f32[1,512]{1,0:T(1,128)S(1)} %bitcast.9, s32[1]{0:T(128)S(6)} %copy.6.live_ref), custom_call_target="tpu_custom_call" | custom-call | tf_op jit(solution)/shard_map/pallas_call | solution.py:420
  44.6 0.8 %broadcast_multiply_fusion = f32[180,720]{1,0:T(8,128)} fusion(f32[180,720]{1,0:T(8,128)S(1)} %shard_map.55), kind=kLoop, calls=%fused_computation | loop fusion | flops 129600 | bytes 1036800 | tf_op jit(solution)/shard_map/mul | solution.py:470
Async XLA Ops:
  0.7 0.7 %copy-start = (s32[512]{0:T(512)S(1)}, s32[512]{0:T(512)}, u32[]{:S(2)}) copy-start(s32[512]{0:T(512)} %param.7) | copy-start | bytes 6148
  1.3 0.7 %copy-start.1 = (f32[512]{0:T(512)S(1)}, f32[512]{0:T(512)}, u32[]{:S(2)}) copy-start(f32[512]{0:T(512)} %param.8) | copy-start | bytes 6148

commit v4 on v3

--- a/solution.py
+++ b/solution.py
@@ -15,14 +15,14 @@
 
 TUNED = (2, 3)
 ORDER = (
-    "F000", "X000", "G00", "N0", "R0", "X010", "X020", "F01", "X001",
-    "H02", "S00", "X011", "N1", "S01", "R1", "H03", "X021", "F10",
-    "S02", "F11", "H12", "T00", "X100", "H13", "N2", "X110", "N3",
-    "T01", "F30", "X120", "H32", "T02", "X101", "R2", "F31", "S10",
-    "X111", "H33", "S11", "X121", "S12", "Y00", "X220", "T10", "Y01",
-    "X221", "T11", "X300", "Y02", "X310", "T12", "R3", "S22", "X320",
-    "Y10", "X301", "S30", "X311", "T22", "Y11", "S31", "X321", "Y12",
-    "S32",
+    "F000", "X000", "N001", "R001", "G00", "X010", "X020", "M0", "R01",
+    "F01", "X001", "H02", "S00", "X011", "N1", "S01", "R1", "H03",
+    "X021", "F10", "S02", "F11", "H12", "T00", "X100", "H13", "N2",
+    "X110", "N3", "T01", "F30", "X120", "H32", "T02", "X101", "R2",
+    "F31", "S10", "X111", "H33", "S11", "X121", "S12", "Y00", "X220",
+    "X221", "T10", "Y01", "X300", "X310", "T11", "X320", "Y02", "X301",
+    "T12", "R3", "X311", "S22", "S30", "X321", "Y10", "T22", "S31",
+    "Y11", "Y12", "S32",
 )
 
 
@@ -58,7 +58,7 @@
     acts_raw, grad_raw, acts, peer_acts, mine, peer, onehot, weight, held,
     send_a, recv_a, send_b, recv_b, send_z, recv_z, recv_y, send_r, recv_r,
     load_sems, grad_sems, acts_sems, w_sems,
-    a_sems, b_sems, z_sems, y_sems, r_sems,
+    a_sems, b_sems, z_sems, y_sems, r_sems, sent, ready,
 ):
     dp = lax.axis_index("dp")
     half = lax.axis_index("tensor")
@@ -134,8 +134,22 @@
         load_acts(step).start()
 
     barrier = pltpu.get_barrier_semaphore()
-    for device in [pair_dev, a_dev, b_dev] + [z_dev(o) for o in targets[:OWN]]:
+    relayed = fars == 2
+    greet = [pair_dev, a_dev, b_dev, z_dev(near)]
+    if not relayed:
+        greet += [z_dev(o) for o in targets[:NEAR]]
+    for device in greet:
         pl.semaphore_signal(barrier, inc=1, device_id=device, device_id_type=MESH)
+
+    def tell_inner(semaphore):
+        @pl.when(leads(0))
+        def _():
+            pl.semaphore_signal(
+                semaphore, inc=1, device_id=z_dev(far(1)), device_id_type=MESH
+            )
+
+    if relayed:
+        tell_inner(barrier)
 
     def turn(row):
         return jnp.broadcast_to(row.astype(jnp.float32), (LANES, slots)).T
@@ -162,15 +176,19 @@
         return remote(
             mine.at[g, :, pl.ds(p * PIECE, PIECE)],
             peer.at[g, :, pl.ds(p * PIECE, PIECE)],
-            (w_sems.at[0, i, p], w_sems.at[1, i, p]), pair_dev,
-        )
-
-    def copy_acts(step):
-        o = targets[step]
+            (sent.at[1], w_sems.at[i, p]), pair_dev,
+        )
+
+    def copy_acts(step, far_half):
+        o, m = targets[step], 1 - mid if far_half else mid
         return remote(
-            acts.at[1 - core, o], peer_acts.at[o],
-            (acts_sems.at[0, step], acts_sems.at[1, step]), pair_dev,
-        )
+            acts.at[1 - core, o, m], peer_acts.at[o, m],
+            (sent.at[0], acts_sems.at[step, far_half]), pair_dev,
+        )
+
+    def send_acts(step):
+        for far_half in (1, 0):
+            copy_acts(step, far_half).start()
 
     def weigh(i, begin, end):
         g = grad_order[i]
@@ -209,12 +227,12 @@
         i = index(step, p)
         return remote(
             send_a.at[i, k], recv_a.at[i, k],
-            (a_sems.at[0, i, k], a_sems.at[1, i, k]), a_dev,
+            (sent.at[2], a_sems.at[i, k]), a_dev,
         )
 
     def copy_b(step, p):
         i = index(step, p)
-        return remote(send_b.at[i], recv_b.at[i], (b_sems.at[0, i], b_sems.at[1, i]), b_dev)
+        return remote(send_b.at[i], recv_b.at[i], (sent.at[3], b_sems.at[i]), b_dev)
 
     def slot(step, p):
         return step // 2 * pieces + p if step < NEAR else fars // 2 * pieces
@@ -222,19 +240,19 @@
     def copy_z(step, p):
         i, j = index(step, p), slot(step, p)
         return remote(
-            send_z.at[i], recv_z.at[j], (z_sems.at[0, i], z_sems.at[1, j]),
+            send_z.at[i], recv_z.at[j], (sent.at[4], z_sems.at[j]),
             z_dev(targets[step]),
         )
 
     def copy_y(step, p):
         i = index(step, p)
         return remote(
-            send_z.at[i], recv_y.at[i], (z_sems.at[0, i], y_sems.at[i]), z_dev(near)
+            send_z.at[i], recv_y.at[i], (sent.at[4], y_sems.at[i]), z_dev(near)
         )
 
     def copy_r(r):
         return remote(
-            send_r.at[r], recv_r.at[r], (r_sems.at[0, r], r_sems.at[1, r]), z_dev(near)
+            send_r.at[r], recv_r.at[r], (sent.at[5], r_sems.at[r]), z_dev(near)
         )
 
     def raw_in(p, q):
@@ -248,8 +266,11 @@
     seen = set()
 
     def need(step, q, pieces_end):
-        wanted = [copy_acts(step)] if ("acts", step) not in seen else []
-        seen.add(("acts", step))
+        wanted = []
+        for far_half in (1,) if q == 0 else (1, 0):
+            if ("acts", step, far_half) not in seen:
+                seen.add(("acts", step, far_half))
+                wanted.append(copy_acts(step, far_half))
         for i in range(1 if q == 0 else 2):
             for p in range(pieces_end):
                 if (i, p) not in seen:
@@ -277,20 +298,24 @@
     def send_first(step, p, k):
         copy_a(step, p, k).start()
 
-    def near_all(q):
-        need(NEAR, q, pieces)
-        total = term(NEAR, q)
-        for p in range(pieces - 1):
-            send_r[p * 4 + q] = total[:, span(p)].astype(jnp.bfloat16)
-        p = pieces - 1
-        part = total[:, span(p)]
-        if q < 2:
-            send_a[index(NEAR, p), q] = part.astype(jnp.bfloat16)
-        else:
-            held[NEAR, q - 2, :, span(p)] = part
-
-    def send_raw(q):
-        for p in range(pieces - 1):
+    def near_some(q, begin=0, end=None):
+        end = pieces if end is None else end
+        need(NEAR, q, end)
+        total = term(NEAR, q, slice(begin * PIECE, end * PIECE))
+        for p in range(begin, end):
+            part = total[:, span(p - begin)]
+            if p < pieces - 1:
+                send_r[p * 4 + q] = part.astype(jnp.bfloat16)
+            elif q < 2:
+                send_a[index(NEAR, p), q] = part.astype(jnp.bfloat16)
+            else:
+                held[NEAR, q - 2, :, span(p)] = part
+
+    def near_rest(q):
+        near_some(q, 1)
+
+    def send_raw(q, begin=0, end=None):
+        for p in range(begin, pieces - 1 if end is None else end):
             copy_r(p * 4 + q).start()
 
     def hold(step, q):
@@ -329,6 +354,8 @@
 
         @pl.when(leads(step))
         def _():
+            if relayed and (step, p) == (0, 0):
+                pl.semaphore_wait(ready, 1)
             copy_y(step, p).wait_recv()
             total = held[step, 1, :, span(p)] + wide(recv_y.at[i])
             send_z[i] = total.astype(jnp.bfloat16)
@@ -337,15 +364,21 @@
     load_grad(0, 0).wait()
     weigh(0, 0, PIECE)
     divide(act_order[0])
-    pl.semaphore_wait(barrier, 2 + outer)
-    copy_acts(act_order[0]).start()
+    if relayed:
+        pl.semaphore_wait(barrier, len(greet) + jnp.where(leads(0), 1, 0))
+        tell_inner(ready)
+    else:
+        pl.semaphore_wait(barrier, len(greet))
+    copy_acts(0, 1).start()
     copy_w(0, 0).start()
+    divide(NEAR)
+    copy_acts(NEAR, 1).start()
     load_grad(0, 1).wait()
     weigh(0, PIECE, columns)
     for p in range(1, pieces):
         copy_w(0, p).start()
-    divide(NEAR)
-    copy_acts(NEAR).start()
+    copy_acts(0, 0).start()
+    copy_acts(NEAR, 0).start()
     for j in range(2):
         load_grad(1, j).wait()
     weigh(1, 0, columns)
@@ -353,28 +386,14 @@
         copy_w(1, p).start()
     for step in act_order[2:]:
         divide(step)
-        copy_acts(step).start()
+        send_acts(step)
+
     actions = {
-        "F": first, "G": first_rest, "X": send_first, "N": near_all, "R": send_raw,
+        "F": first, "G": first_rest, "X": send_first, "N": near_some, "M": near_rest, "R": send_raw,
         "H": hold, "S": second, "T": third, "Y": forward,
     }
     for name, *where in plan(fars, pieces):
         actions[name](*where)
-
-    for step in range(outer):
-        for p in range(pieces):
-            if step == NEAR and p < pieces - 1:
-                continue
-            copy_a(step, p, 0).wait_send()
-            copy_a(step, p, 1).wait_send()
-            if step < NEAR:
-                copy_b(step, p).wait_send()
-        copy_acts(step).wait_send()
-    for r in range(raws):
-        copy_r(r).wait_send()
-    for i in range(2):
-        for p in range(pieces):
-            copy_w(i, p).wait_send()
 
     for p in range(pieces):
         i = index(OWN, p)
@@ -397,12 +416,13 @@
             copy_z(NEAR, p).wait_recv()
             total = total + wide(recv_z.at[slot(NEAR, p)])
         out_ref[:, p * PIECE : p * PIECE + width] = total[:, :width]
-        copy_b(OWN, p).wait_send()
-    for step in range(fars):
-        for p in range(pieces):
-            copy_z(step, p).wait_send()
-    copy_b(NEAR, pieces - 1).wait_send()
-    copy_z(NEAR, pieces - 1).wait_send()
+
+    def settle(ref, k):
+        remote(ref, ref, (sent.at[k], sent.at[k]), pair_dev).wait_send()
+
+    settle(peer_acts, 0)
+    for k, ref in enumerate((mine, send_a, send_b, send_z, send_r)):
+        settle(ref, k + 1)
 
 
 def shards(expert_act, grad_out, slot_token, slot_prob, live_count):
@@ -449,13 +469,15 @@
             pltpu.VMEM((raws, rows, PIECE), bf16),
             dma((outer,)),
             dma((2, 2)),
-            dma((2, outer)),
-            dma((2, 2, pieces)),
-            dma((2, count, 2)),
-            dma((2, count)),
-            dma((2, count - pieces)),
-            dma((count - pieces,)),
-            dma((2, raws)),
+            dma((outer, 2)),
+            dma((2, pieces)),
+            dma((count, 2)),
+            dma((count,)),
+            dma(((outer - 2) // 2 * pieces + 1,)),
+            dma((count - 1 - pieces,)),
+            dma((raws,)),
+            dma((6,)),
+            pltpu.SemaphoreType.REGULAR,
         ],
         compiler_params=pltpu.CompilerParams(
             collective_id=0, has_side_effects=True, vmem_limit_bytes=53 * 2**20

time: 45.6 us -> 43.5 us (0.954)
  Pallas kernels: 42.6 us -> 40.4 us
    pallas_call x1, Pallas kernels: 42.6 us -> 40.4 us  [shards(): pl.pallas_call(functools.partial(kernel, outer), out_shape=jax.ShapeDtype...]
where the time goes in v4:
time: 43.5 us; the launch traced here: 43.3 us
  Pallas kernels  40.4 us (93%)
  local copies, waits for them, and re-layouts  1.36 us (3%)
  other arithmetic  0.85 us (2%)
  between operations  0.67 us (2%)
    pallas_call x1, Pallas kernels, shards(): pl.pallas_call(functools.partial(kernel, outer), out_shape=jax.ShapeDtype...  40.4 us
    unnamed x4, local copies, waits for them, and re-layouts  1.36 us

profile of v4, /device:TPU:0, one launch (start us, length us, event | category | flops | bytes accessed | tf_op | source)
XLA Modules:
  0.0 43.3 jit_solution(14856825186553149270)
XLA Ops:
  0.7 0.0 copy-start
  0.7 0.7 %copy-done = s32[512]{0:T(512)S(1)} copy-done((s32[512]{0:T(512)S(1)}, s32[512]{0:T(512)}, u32[]{:S(2)}) %copy-start) | copy-done | bytes 2072
  1.3 0.0 copy-start.1
  1.3 0.7 %copy-done.1 = f32[512]{0:T(512)S(1)} copy-done((f32[512]{0:T(512)S(1)}, f32[512]{0:T(512)}, u32[]{:S(2)}) %copy-start.1) | copy-done | bytes 2072
  2.0 40.4 %shard_map.55 = f32[180,720]{1,0:T(8,128)S(1)} custom-call(bf16[4,720,512]{2,1,0:T(8,128)(2,1)} %bitcast.10, bf16[2,720,1024]{2,1,0:T(8,128)(2,1)} %bitcast.11, s32[1,512]{1,0:T(1,128)S(1)} %bitcast.8, f32[1,512]{1,0:T(1,128)S(1)} %bitcast.9, s32[1]{0:T(128)S(6)} %copy.6.live_ref), custom_call_target="tpu_custom_call" | custom-call | tf_op jit(solution)/shard_map/pallas_call | solution.py:440
  42.4 0.8 %broadcast_multiply_fusion = f32[180,720]{1,0:T(8,128)} fusion(f32[180,720]{1,0:T(8,128)S(1)} %shard_map.55), kind=kLoop, calls=%fused_computation | loop fusion | flops 129600 | bytes 1036800 | tf_op jit(solution)/shard_map/mul | solution.py:492
Async XLA Ops:
  0.7 0.7 %copy-start = (s32[512]{0:T(512)S(1)}, s32[512]{0:T(512)}, u32[]{:S(2)}) copy-start(s32[512]{0:T(512)} %param.7) | copy-start | bytes 6148
  1.3 0.7 %copy-start.1 = (f32[512]{0:T(512)S(1)}, f32[512]{0:T(512)}, u32[]{:S(2)}) copy-start(f32[512]{0:T(512)} %param.8) | copy-start | bytes 6148

commit v5 on v4

--- a/solution.py
+++ b/solution.py
@@ -15,14 +15,14 @@
 
 TUNED = (2, 3)
 ORDER = (
-    "F000", "X000", "N001", "R001", "G00", "X010", "X020", "M0", "R01",
-    "F01", "X001", "H02", "S00", "X011", "N1", "S01", "R1", "H03",
-    "X021", "F10", "S02", "F11", "H12", "T00", "X100", "H13", "N2",
-    "X110", "N3", "T01", "F30", "X120", "H32", "T02", "X101", "R2",
-    "F31", "S10", "X111", "H33", "S11", "X121", "S12", "Y00", "X220",
-    "X221", "T10", "Y01", "X300", "X310", "T11", "X320", "Y02", "X301",
-    "T12", "R3", "X311", "S22", "S30", "X321", "Y10", "T22", "S31",
-    "Y11", "Y12", "S32",
+    "F000", "X000", "N001", "R001", "W0", "G00", "X010", "X020", "W1",
+    "F010", "X001", "M0", "X220", "R01", "D", "G01", "X011", "H02",
+    "S00", "N1", "S01", "R1", "H03", "X021", "F10", "S02", "F11",
+    "H12", "T00", "X100", "H13", "N2", "X110", "N3", "T01", "X120",
+    "F30", "H32", "X101", "T02", "R2", "F31", "S10", "X111", "X121",
+    "H33", "S11", "S12", "X221", "Y00", "X300", "X310", "T10", "Y01",
+    "X320", "T11", "Y02", "X301", "X311", "T12", "S22", "R3", "S30",
+    "X321", "T22", "Y10", "S31", "Y11", "Y12", "S32",
 )
 
 
@@ -30,7 +30,8 @@
     if (fars, pieces) == TUNED:
         return [(token[0], *map(int, token[1:])) for token in ORDER]
     near, own, every = fars, fars + 1, range(pieces)
-    steps = [("F", 0, 0, p) for p in every] + [("F", 0, 1, p) for p in every]
+    steps = [("W", 0), ("W", 1), ("D",)]
+    steps += [("F", 0, k, p) for k in range(2) for p in every]
     steps += [("X", 0, p, k) for k in range(2) for p in every]
     steps += [(name, q) for q in range(4) for name in "NR"]
     steps += [("X", near, pieces - 1, k) for k in range(2)]
@@ -379,18 +380,22 @@
         copy_w(0, p).start()
     copy_acts(0, 0).start()
     copy_acts(NEAR, 0).start()
-    for j in range(2):
-        load_grad(1, j).wait()
-    weigh(1, 0, columns)
-    for p in range(pieces):
-        copy_w(1, p).start()
-    for step in act_order[2:]:
-        divide(step)
-        send_acts(step)
+
+    def weigh_mine(part):
+        begin, end = (0, 1) if part == 0 else (1, pieces)
+        load_grad(1, part).wait()
+        weigh(1, begin * PIECE, min(end * PIECE, columns))
+        for p in range(begin, end):
+            copy_w(1, p).start()
+
+    def divide_rest():
+        for step in act_order[2:]:
+            divide(step)
+            send_acts(step)
 
     actions = {
         "F": first, "G": first_rest, "X": send_first, "N": near_some, "M": near_rest, "R": send_raw,
-        "H": hold, "S": second, "T": third, "Y": forward,
+        "W": weigh_mine, "D": divide_rest, "H": hold, "S": second, "T": third, "Y": forward,
     }
     for name, *where in plan(fars, pieces):
         actions[name](*where)

time: 43.5 us -> 42.8 us (0.984)
  Pallas kernels: 40.4 us -> 39.8 us
    pallas_call x1, Pallas kernels: 40.4 us -> 39.8 us  [shards(): pl.pallas_call(functools.partial(kernel, outer), out_shape=jax.ShapeDtype...]
where the time goes in v5:
time: 42.8 us; the launch traced here: 42.7 us
  Pallas kernels  39.8 us (93%)
  local copies, waits for them, and re-layouts  1.36 us (3%)
  other arithmetic  0.85 us (2%)
  between operations  0.67 us (2%)
    pallas_call x1, Pallas kernels, shards(): pl.pallas_call(functools.partial(kernel, outer), out_shape=jax.ShapeDtype...  39.8 us
    unnamed x4, local copies, waits for them, and re-layouts  1.36 us

profile of v5, /device:TPU:0, one launch (start us, length us, event | category | flops | bytes accessed | tf_op | source)
XLA Modules:
  0.0 42.7 jit_solution(6108936757406486683)
XLA Ops:
  0.7 0.0 copy-start
  0.7 0.7 %copy-done = s32[512]{0:T(512)S(1)} copy-done((s32[512]{0:T(512)S(1)}, s32[512]{0:T(512)}, u32[]{:S(2)}) %copy-start) | copy-done | bytes 2072
  1.3 0.0 copy-start.1
  1.3 0.7 %copy-done.1 = f32[512]{0:T(512)S(1)} copy-done((f32[512]{0:T(512)S(1)}, f32[512]{0:T(512)}, u32[]{:S(2)}) %copy-start.1) | copy-done | bytes 2072
  2.0 39.8 %shard_map.55 = f32[180,720]{1,0:T(8,128)S(1)} custom-call(bf16[4,720,512]{2,1,0:T(8,128)(2,1)} %bitcast.10, bf16[2,720,1024]{2,1,0:T(8,128)(2,1)} %bitcast.11, s32[1,512]{1,0:T(1,128)S(1)} %bitcast.8, f32[1,512]{1,0:T(1,128)S(1)} %bitcast.9, s32[1]{0:T(128)S(6)} %copy.6.live_ref), custom_call_target="tpu_custom_call" | custom-call | tf_op jit(solution)/shard_map/pallas_call | solution.py:445
  41.8 0.8 %broadcast_multiply_fusion = f32[180,720]{1,0:T(8,128)} fusion(f32[180,720]{1,0:T(8,128)S(1)} %shard_map.55), kind=kLoop, calls=%fused_computation | loop fusion | flops 129600 | bytes 1036800 | tf_op jit(solution)/shard_map/mul | solution.py:497
Async XLA Ops:
  0.7 0.7 %copy-start = (s32[512]{0:T(512)S(1)}, s32[512]{0:T(512)}, u32[]{:S(2)}) copy-start(s32[512]{0:T(512)} %param.7) | copy-start | bytes 6148
  1.3 0.7 %copy-start.1 = (f32[512]{0:T(512)S(1)}, f32[512]{0:T(512)}, u32[]{:S(2)}) copy-start(f32[512]{0:T(512)} %param.8) | copy-start | bytes 6148
